TPU v7x, 32 devices: a whole 2x2x4 slice. The times are simulated.
32 devices in a mesh: path: 8 (over y, x, core), tm: 4 (over z).
Axes of the slice: x: 2, y: 2, z: 4, core: 2. Of those that a mesh axis runs over, the one named last changes fastest.
Arguments:
- increments: bfloat16 [8192, 32, 1000], P(('path', 'tm')), may hold values from -6 to 6
- level_table: int32 [4096], replicated, may hold values from 0 to 4, as said below
- time_table: int32 [4096], replicated, may hold values from 0 to 31, as said below
Outputs:
- value_est: float32 [32], P('tm')
- grad_est: float32 [32, 1000], P('tm')
Inputs may be any that keep to these rules, and one draw needn't show every extreme that they name: `level_table`: never falls from one block to the next. `time_table`: split the 32 time points into as many runs of consecutive points as the tm axis has devices; the 128 consecutive entries of each device fall equally into every run.
All inputs are finite; a program needn't handle non-finite values.
Results may differ from a plain program's by a relative error of at most 0.0003.
The roundings to bfloat16 on the way count: a program that leaves them out, or rounds other values in their place, can miss the bound.
Values may be sent and summed in bfloat16 or wider, within the bound.
No kernel may reach another device: no remote copies, remote signals or barrier semaphores. Data moves between devices by JAX's collectives and lax.ppermute only.
A program may use at most 128 MiB of HBM per device.

v0:
```python
import jax
import jax.numpy as jnp
from jax import lax
from jax.sharding import PartitionSpec as P

LEVELS = 5
BLOCK = 2
horizon = 0.3


def stride_weights(levels, starts, steps_k, step_len):
    steps = jnp.arange(steps_k)
    fine_stride = jnp.power(2, LEVELS - 1 - levels).astype(jnp.int32)
    coarse = fine_stride * 2
    live_steps = steps[None, :] >= starts[:, None]
    on_fine = steps[None, :] % fine_stride[:, None] == 0
    on_coarse = (steps[None, :] % coarse[:, None] == 0) & (levels[:, None] > 0)
    term = fine_stride[:, None] * on_fine.astype(jnp.int32) - coarse[:, None] * on_coarse.astype(
        jnp.int32
    )
    return step_len * (live_steps.astype(jnp.float32) * term.astype(jnp.float32))


def terminal(incr, starts):
    steps_k = incr.shape[1]
    width = incr.shape[2]
    step_len = horizon / steps_k
    steps = jnp.arange(steps_k)
    live_steps = (steps[None, :] >= starts[:, None]).astype(jnp.bfloat16)
    end_point = jnp.sqrt(step_len) * jnp.einsum(
        "pi,pid->pd", live_steps, incr, preferred_element_type=jnp.float32
    )
    remaining = horizon - starts.astype(jnp.float32) * step_len
    scaled = end_point / remaining[:, None]
    end_value = 1.0 / (2.0 + 0.4 * jnp.sum(end_point * end_point, axis=1) / width)
    return (scaled, end_value)


def partial_sums(path_total, scaled, row_index, path_share, row_count):
    select = (row_index[:, None] == jnp.arange(row_count)[None, :]).astype(jnp.float32)
    select = select * (path_share * path_total)[:, None]
    return (jnp.sum(select, axis=0), jnp.dot(select.T, scaled, precision=lax.Precision.HIGHEST))


def first_terms(incr, levels, starts, path_share, row_count, offset):
    scaled, end_value = terminal(incr, starts)
    path_total = end_value * (levels == 0).astype(jnp.float32)
    return partial_sums(path_total, scaled, starts - offset, path_share, row_count)


def second_terms(incr, levels, starts, path_share, value_one, grad_low, row_count, offset):
    paths, steps_k, width = incr.shape
    step_len = horizon / steps_k
    scaled, end_value = terminal(incr, starts)
    inner_dots = jnp.dot(
        incr.reshape(paths * steps_k, width), grad_low.T, preferred_element_type=jnp.float32
    ).reshape(paths, steps_k, steps_k)
    steps = jnp.arange(steps_k)
    window = (steps[None, :, None] >= starts[:, None, None]) & (
        steps[None, :, None] < steps[None, None, :]
    )
    estimate = value_one[None, :] + jnp.sqrt(step_len) * jnp.sum(
        inner_dots * window.astype(jnp.float32), axis=1
    )
    drift_term = estimate - estimate * estimate * estimate
    weights = stride_weights(levels, starts, steps_k, step_len)
    path_total = end_value * (levels == 0).astype(jnp.float32) + jnp.sum(
        weights * drift_term, axis=1
    )
    return partial_sums(path_total, scaled, starts - offset, path_share, row_count)


def shards(increments, level_table, time_table):
    groups = lax.axis_size("tm")
    devices = lax.axis_size("path") * groups
    my_index = lax.axis_index("path") * groups + lax.axis_index("tm")
    blk_dev = level_table.shape[0] // devices
    steps_k = increments.shape[1]
    lvl_hot = (level_table[:, None] == jnp.arange(LEVELS)[None, :]).astype(jnp.float32)
    time_hot = (time_table[:, None] == jnp.arange(steps_k)[None, :]).astype(jnp.float32)
    counts = jnp.dot(lvl_hot.T, time_hot, precision=lax.Precision.HIGHEST)
    own_levels = lax.dynamic_slice_in_dim(level_table, my_index * blk_dev, blk_dev)
    own_times = lax.dynamic_slice_in_dim(time_table, my_index * blk_dev, blk_dev)
    lvl_path = jnp.repeat(own_levels, BLOCK)
    time_path = jnp.repeat(own_times, BLOCK)
    path_share = 1.0 / (BLOCK * counts[lvl_path, time_path])
    value_one, grad_one = lax.psum(
        first_terms(increments, lvl_path, time_path, path_share, steps_k, 0), ("path", "tm")
    )
    grad_low = grad_one.astype(jnp.bfloat16)
    value_part, grad_part = lax.psum_scatter(
        second_terms(increments, lvl_path, time_path, path_share, value_one, grad_low, steps_k, 0),
        "tm",
        scatter_dimension=0,
        tiled=True,
    )
    value_est, grad_est = lax.psum((value_part, grad_part), "path")
    return (value_est, grad_est)


def solution(mesh):
    placed = (P(("path", "tm"), None, None), P(), P())
    return jax.shard_map(
        shards, mesh=mesh, in_specs=placed, out_specs=(P("tm"), P("tm", None)), check_vma=False
    )
```

profile of v0, /device:TPU:0, one launch (start us, length us, event | category | flops | bytes accessed | tf_op | source)
XLA Modules:
  0.0 158.6 jit_solution(13497619476478879534)
XLA Ops:
  7.2 0.0 reduce-scatter.2.cloned.1.call-start
  7.2 0.8 broadcast_compare_fusion
  8.0 0.8 dynamic_slice.6
  8.7 0.9 fusion
  9.7 0.1 broadcast_in_dim.22
  9.8 0.2 reshape.283
  9.9 0.1 eq.74
  10.1 0.1 broadcast_in_dim.23
  10.2 0.1 reshape.282
  10.4 23.5 %copy.11 = bf16[256,32,1000]{2,1,0:T(8,128)(2,1)} copy(bf16[256,32,1000]{0,2,1:T(8,128)(2,1)} %param.5) | data formatting | bytes 32768000 | tf_op args[0]
  33.9 7.1 %multiply_reduce_fusion = f32[256,1000]{0,1:T(8,128)S(1)} fusion(bf16[256,32,1000]{0,2,1:T(8,128)(2,1)} %param.5, f32[256,32]{0,1:T(8,128)S(1)} %get-tuple-element.18), kind=kLoop, calls=%fused_computation.1 | loop fusion | flops 24320000 | bytes 17440768 | tf_op jit(solution)/shard_map/pi,pid->pd/dot_general | solution.py:30
  41.0 0.2 multiply_reduce_fusion.1
  41.1 0.1 broadcast_in_dim.24
  41.2 0.1 eq.85
  41.4 1.4 gather_fusion
  42.8 0.1 select_reduce_fusion.2
  42.9 1.0 fusion.2
  43.9 0.0 copy-start
  43.9 44.4 %all-reduce.1 = (bf16[32,1000]{1,0:T(8,128)(2,1)S(1)}, f32[32]{0:T(128)S(1)}) all-reduce(f32[32,1000]{1,0:T(8,128)S(1)} %fusion.2, f32[32]{0:T(128)S(1)} %select_reduce_fusion.2), channel_id=1, replica_groups=mesh['path'=8,'tm'=4] {'path','tm'}, use_global_device_ids=true, to_apply=%region_3.5 | all-reduce | flops 32032 | bytes 192256 | tf_op jit(solution)/shard_map/psum | solution.py:87
  88.3 10.7 %convolution_bitcast_fusion = f32[8192,32]{0,1:T(8,128)S(1)} fusion(bf16[8192,1000]{1,0:T(8,128)(2,1)} %bitcast.11, bf16[32,1000]{1,0:T(8,128)(2,1)S(1)} %get-tuple-element.3), kind=kOutput, calls=%fused_computation.2 | convolution fusion | flops 524288000 | bytes 17496576 | tf_op jit(solution)/shard_map/dot_general | solution.py:55
  99.0 2.7 %reshape.285 = f32[256,32,32]{1,0,2:T(8,128)} reshape(f32[8192,32]{0,1:T(8,128)S(1)} %convolution_bitcast_fusion) | data formatting | bytes 2097152 | tf_op jit(solution)/shard_map/reshape | solution.py:57
  101.7 0.1 copy.10
  101.9 0.1 broadcast.622
  102.0 0.1 reshape.301
  102.1 0.1 broadcast.629
  102.2 0.1 reshape.303
  102.4 0.1 broadcast_in_dim.28
  102.5 0.1 ne.146
  102.6 0.1 broadcast.601
  102.7 0.1 reshape.291
  102.8 0.1 broadcast.611
  102.9 0.1 reshape.297
  103.1 0.1 broadcast_in_dim.29
  103.2 0.2 select_n.157
  103.3 0.1 broadcast_in_dim.30
  103.4 0.1 gt.14
  103.6 3.3 %select_reduce_fusion = f32[256,32]{0,1:T(8,128)S(1)} fusion(f32[256,32,32]{1,0,2:T(8,128)} %reshape.285, pred[32,32]{0,1:T(8,128)(4,1)S(1)} %iota_compare_fusion.8, pred[256,32]{1,0:T(8,128)(4,1)S(1)} %copy.10), kind=kLoop, calls=%fused_computation.3 | loop fusion | flops 778240 | bytes 1090560 | tf_op jit(solution)/shard_map/reduce_sum | solution.py:62
  106.9 0.7 fusion.9
  107.6 1.6 %fusion.1 = f32[32,1000]{1,0:T(8,128)} fusion(f32[256,1000]{0,1:T(8,128)S(1)} %multiply_reduce_fusion, f32[256]{0:T(256)S(1)} %get-tuple-element.26, f32[256]{0:T(256)S(1)} %add_multiply_fusion, s32[256]{0:T(256)S(1)} %eq.74), kind=kOutput, calls=%fused_computation.8 | convolution fusion | flops 98832384 | bytes 1155072 | tf_op jit(solution)/shard_map/dot_general | solution.py:42
  109.3 0.0 reduce-scatter.2.cloned.1.call-update
  109.3 0.0 copy-done
  109.3 0.6 dynamic-slice
  110.5 0.1 select_reduce_fusion.1
  110.7 10.6 %all-reduce = f32[32]{0:T(128)S(1)} all-reduce(f32[32]{0:T(128)S(1)} %select_reduce_fusion.1), channel_id=2, replica_groups=mesh['path'=8,'tm'=4] {'tm'}, use_global_device_ids=true, to_apply=%region_7.9.clone | all-reduce | flops 32 | bytes 256
  121.2 0.1 dynamic-slice.1
  121.3 6.6 %reduce-scatter.2.cloned.1.call-done = f32[8,1000]{1,0:T(8,128)} async-done(((f32[32,1000]{1,0:T(8,128)}), f32[8,1000]{1,0:T(8,128)}) %reduce-scatter.2.cloned.1.call-update) | async-done | bytes 32016 | tf_op jit(solution)/shard_map/reduce_scatter | solution.py:91
  127.9 23.9 %all-reduce.2 = (f32[8]{0:T(128)}, f32[8,1000]{1,0:T(8,128)}) all-reduce(f32[8]{0:T(128)S(1)} %dynamic-slice.1, f32[8,1000]{1,0:T(8,128)} %reduce-scatter.2.cloned.1.call-done), channel_id=1, replica_groups=mesh['path'=8,'tm'=4] {'path'}, use_global_device_ids=true, to_apply=%region_8.10 | all-reduce | flops 8008 | bytes 64064 | tf_op jit(solution)/shard_map/psum | solution.py:97
  (12 shorter events, 0.2 us)
Async XLA Ops:
  7.2 120.7 %reduce-scatter.2.cloned.1.call-start = ((), (), s32[]{:S(2)}) async-start(), calls=%async_computation.1 | async-start | bytes 163840 | tf_op jit(solution)/shard_map/reduce_scatter | solution.py:91
  43.9 65.4 %copy-start = (u32[32]{0:T(128)S(1)}, u32[32]{0:T(128)}, u32[]{:S(2)}) copy-start(u32[32]{0:T(128)} %constant.92) | copy-start | bytes 388
Sparse Core Ops, SparseCore 0:
  109.4 18.4 reduce-scatter.1
where the time goes:
time: 160 us; the launch traced here: 159 us
  blocking collectives  78.9 us (49%)
  local copies, waits for them, and re-layouts  31.6 us (20%)
  between operations  14.9 us (9%)
  matrix products  14.2 us (9%)
  other arithmetic  12.4 us (8%)
  waiting for transfers between devices  6.62 us (4%)
    psum x1, blocking collectives, shards(): lax.psum(first_terms(increments, lvl_path, time_path, path_share, steps_k...  44.4 us
    unnamed x5, local copies, waits for them, and re-layouts  24.1 us
    psum x1, blocking collectives, shards(): value_est, grad_est = lax.psum((value_part, grad_part), 'path')  23.9 us
    dot_general x1, matrix products, second_terms(): jnp.dot(incr.reshape(paths * steps_k, width), grad_low.T, preferred_eleme...  10.7 us
    unnamed x1, blocking collectives  10.6 us
    dot_general x1, other arithmetic, terminal(): jnp.einsum('pi,pid->pd', live_steps, incr, preferred_element_type=jnp.flo...  7.07 us
    reduce_scatter x1, waiting for transfers between devices, shards(): lax.psum_scatter(second_terms(increments, lvl_path, time_path, path_share...  6.6 us
    reduce_sum x1, other arithmetic, second_terms(): jnp.sum(inner_dots * window.astype(jnp.float32), axis=1)  3.35 us
  transfers between devices with their start and end apart: 1, of which 1 were waited for; matrix products, arithmetic and copies ran while one was open for 0% of the time, Pallas kernels for 0%

commit v1 on v0

--- a/solution.py
+++ b/solution.py
@@ -85,7 +85,7 @@
     time_path = jnp.repeat(own_times, BLOCK)
     path_share = 1.0 / (BLOCK * counts[lvl_path, time_path])
     value_one, grad_one = lax.psum(
-        first_terms(increments, lvl_path, time_path, path_share, steps_k, 0), ("path", "tm")
+        lax.psum(first_terms(increments, lvl_path, time_path, path_share, steps_k, 0), "path"), "tm"
     )
     grad_low = grad_one.astype(jnp.bfloat16)
     value_part, grad_part = lax.psum_scatter(

time: 160 us -> 166 us (1.038)
  waiting for transfers between devices: 6.62 us -> 22.3 us
  blocking collectives: 78.9 us -> 69.2 us
    psum x1, blocking collectives: 44.4 us -> 15.2 us  [shards(): lax.psum(first_terms(increments, lvl_path, time_path, path_share, steps_k...]
    psum x0 -> x1, blocking collectives: none -> 21.8 us  [shards(): lax.psum(lax.psum(first_terms(increments, lvl_path, time_path, path_share...]
    psum x0 -> x1, waiting for transfers between devices: none -> 15.6 us  [shards(): lax.psum(first_terms(increments, lvl_path, time_path, path_share, steps_k...]
    unnamed x1, blocking collectives: 10.6 us -> 8.37 us
  transfers between devices with their start and end apart: 1 -> 2, of which waited for: 1 -> 2; matrix products, arithmetic and copies ran while one was open for 0% -> 16% of each run, Pallas kernels for 0% -> 0%
where the time goes in v1:
time: 166 us; the launch traced here: 165 us
  blocking collectives  69.2 us (42%)
  local copies, waits for them, and re-layouts  31.6 us (19%)
  waiting for transfers between devices  22.3 us (13%)
  matrix products  14.9 us (9%)
  between operations  14.9 us (9%)
  other arithmetic  12.4 us (7%)
    unnamed x5, local copies, waits for them, and re-layouts  24.1 us
    psum x1, blocking collectives, shards(): value_est, grad_est = lax.psum((value_part, grad_part), 'path')  23.9 us
    psum x1, blocking collectives, shards(): lax.psum(lax.psum(first_terms(increments, lvl_path, time_path, path_share...  21.8 us
    psum x1, waiting for transfers between devices, shards(): lax.psum(first_terms(increments, lvl_path, time_path, path_share, steps_k...  15.6 us
    psum x1, blocking collectives, shards(): lax.psum(first_terms(increments, lvl_path, time_path, path_share, steps_k...  15.2 us
    dot_general x1, matrix products, second_terms(): jnp.dot(incr.reshape(paths * steps_k, width), grad_low.T, preferred_eleme...  10.7 us
    unnamed x1, blocking collectives  8.37 us
    dot_general x1, other arithmetic, terminal(): jnp.einsum('pi,pid->pd', live_steps, incr, preferred_element_type=jnp.flo...  7.07 us
  transfers between devices with their start and end apart: 2, of which 2 were waited for; matrix products, arithmetic and copies ran while one was open for 16% of the time, Pallas kernels for 0%

profile of v1, /device:TPU:0, one launch (start us, length us, event | category | flops | bytes accessed | tf_op | source)
XLA Modules:
  0.0 165.3 jit_solution(1685073692375863786)
XLA Ops:
  7.2 0.0 all-reduce.5.cloned.1.call-start
  7.2 0.8 broadcast_compare_fusion
  8.0 0.8 dynamic_slice.6
  8.7 0.9 fusion
  9.7 0.1 broadcast_in_dim.22
  9.8 0.2 reshape.283
  9.9 0.1 eq.74
  10.1 0.1 broadcast_in_dim.23
  10.2 0.1 reshape.282
  10.3 7.1 %multiply_reduce_fusion = f32[256,1000]{0,1:T(8,128)S(1)} fusion(bf16[256,32,1000]{0,2,1:T(8,128)(2,1)} %param.5, f32[256,32]{0,1:T(8,128)S(1)} %get-tuple-element.18), kind=kLoop, calls=%fused_computation.1 | loop fusion | flops 24320000 | bytes 17440768 | tf_op jit(solution)/shard_map/pi,pid->pd/dot_general | solution.py:30
  17.4 0.2 multiply_reduce_fusion.1
  17.6 0.1 broadcast_in_dim.24
  17.7 0.1 eq.85
  17.8 1.4 gather_fusion
  19.3 1.6 fusion.2
  20.9 0.0 all-reduce.5.cloned.1.call-update
  20.9 0.0 reduce-scatter.2.cloned.1.call-start
  21.0 0.1 select_reduce_fusion.2
  21.1 23.5 %copy.11 = bf16[256,32,1000]{2,1,0:T(8,128)(2,1)} copy(bf16[256,32,1000]{0,2,1:T(8,128)(2,1)} %param.5) | data formatting | bytes 32768000 | tf_op args[0]
  44.6 0.0 copy-start
  44.7 15.2 %psum.42 = f32[32]{0:T(128)S(1)} all-reduce(f32[32]{0:T(128)S(1)} %select_reduce_fusion.2), channel_id=1, replica_groups=mesh['path'=8,'tm'=4] {'path'}, use_global_device_ids=true, to_apply=%region_2.4 | all-reduce | flops 32 | bytes 256 | tf_op jit(solution)/shard_map/psum | solution.py:88
  59.8 0.1 copy.10
  60.0 0.1 broadcast.622
  60.1 0.2 reshape.301
  60.2 0.1 broadcast.629
  60.3 0.1 reshape.303
  60.4 0.1 broadcast_in_dim.28
  60.5 0.1 ne.146
  60.7 0.1 broadcast.601
  60.8 0.1 reshape.291
  60.9 0.1 broadcast.611
  61.0 0.1 reshape.297
  61.2 0.1 broadcast_in_dim.29
  61.3 0.2 select_n.157
  61.4 0.1 broadcast_in_dim.30
  61.5 0.1 gt.14
  61.7 15.6 %all-reduce.5.cloned.1.call-done = f32[32,1000]{1,0:T(8,128)} async-done(((f32[32,1000]{1,0:T(8,128)}), f32[32,1000]{1,0:T(8,128)}) %all-reduce.5.cloned.1.call-update) | async-done | bytes 128016 | tf_op jit(solution)/shard_map/psum | solution.py:88
  77.3 21.8 %all-reduce.2 = (bf16[32,1000]{1,0:T(8,128)(2,1)S(1)}, f32[32]{0:T(128)S(1)}) all-reduce(f32[32,1000]{1,0:T(8,128)} %all-reduce.5.cloned.1.call-done, f32[32]{0:T(128)S(1)} %psum.42), channel_id=1, replica_groups=mesh['path'=8,'tm'=4] {'tm'}, use_global_device_ids=true, to_apply=%region_5.7 | all-reduce | flops 32032 | bytes 192256 | tf_op jit(solution)/shard_map/psum | solution.py:87
  99.1 10.7 %convolution_bitcast_fusion = f32[8192,32]{0,1:T(8,128)S(1)} fusion(bf16[8192,1000]{1,0:T(8,128)(2,1)} %bitcast.11, bf16[32,1000]{1,0:T(8,128)(2,1)S(1)} %get-tuple-element.5), kind=kOutput, calls=%fused_computation.2 | convolution fusion | flops 524288000 | bytes 17496576 | tf_op jit(solution)/shard_map/dot_general | solution.py:55
  109.8 2.7 %reshape.285 = f32[256,32,32]{1,0,2:T(8,128)} reshape(f32[8192,32]{0,1:T(8,128)S(1)} %convolution_bitcast_fusion) | data formatting | bytes 2097152 | tf_op jit(solution)/shard_map/reshape | solution.py:57
  112.5 3.3 %select_reduce_fusion = f32[256,32]{0,1:T(8,128)S(1)} fusion(f32[256,32,32]{1,0,2:T(8,128)} %reshape.285, pred[32,32]{0,1:T(8,128)(4,1)S(1)} %iota_compare_fusion.8, pred[256,32]{1,0:T(8,128)(4,1)S(1)} %copy.10), kind=kLoop, calls=%fused_computation.3 | loop fusion | flops 778240 | bytes 1090560 | tf_op jit(solution)/shard_map/reduce_sum | solution.py:62
  115.8 0.7 fusion.9
  116.5 1.6 fusion.1
  118.1 0.0 reduce-scatter.2.cloned.1.call-update
  118.2 0.0 copy-done
  118.2 0.6 dynamic-slice
  119.4 0.1 select_reduce_fusion.1
  119.5 8.4 %all-reduce = f32[32]{0:T(128)S(1)} all-reduce(f32[32]{0:T(128)S(1)} %select_reduce_fusion.1), channel_id=2, replica_groups=mesh['path'=8,'tm'=4] {'tm'}, use_global_device_ids=true, to_apply=%region_9.11.clone | all-reduce | flops 32 | bytes 256
  127.9 0.1 dynamic-slice.1
  128.0 6.7 %reduce-scatter.2.cloned.1.call-done = f32[8,1000]{1,0:T(8,128)} async-done(((f32[32,1000]{1,0:T(8,128)}), f32[8,1000]{1,0:T(8,128)}) %reduce-scatter.2.cloned.1.call-update) | async-done | bytes 32016 | tf_op jit(solution)/shard_map/reduce_scatter | solution.py:91
  134.6 23.9 %all-reduce.1 = (f32[8]{0:T(128)}, f32[8,1000]{1,0:T(8,128)}) all-reduce(f32[8]{0:T(128)S(1)} %dynamic-slice.1, f32[8,1000]{1,0:T(8,128)} %reduce-scatter.2.cloned.1.call-done), channel_id=1, replica_groups=mesh['path'=8,'tm'=4] {'path'}, use_global_device_ids=true, to_apply=%region_10.12 | all-reduce | flops 8008 | bytes 64064 | tf_op jit(solution)/shard_map/psum | solution.py:97
  (13 shorter events, 0.2 us)
Async XLA Ops:
  7.2 70.1 %all-reduce.5.cloned.1.call-start = ((), (), s32[]{:S(2)}) async-start(), calls=%async_computation.1 | async-start | bytes 262144 | tf_op jit(solution)/shard_map/psum | solution.py:88
  20.9 113.7 %reduce-scatter.2.cloned.1.call-start = ((), (), s32[]{:S(2)}) async-start(), calls=%async_computation.2 | async-start | bytes 163840 | tf_op jit(solution)/shard_map/reduce_scatter | solution.py:91
  44.6 73.6 %copy-start = (u32[32]{0:T(128)S(1)}, u32[32]{0:T(128)}, u32[]{:S(2)}) copy-start(u32[32]{0:T(128)} %constant.92) | copy-start | bytes 388
Sparse Core Ops, SparseCore 0:
  21.1 56.1 all-reduce.4
  118.3 16.2 reduce-scatter.1
